TPU v7x, 16 devices: a 4x2x1 block of a 4x4x8 slice. The times are simulated.
16 devices in a mesh: ens: 2 (over y, z), sp: 8 (over x, core).
Axes of the slice: x: 4, y: 2, z: 1, core: 2. Of those that a mesh axis runs over, the one named last changes fastest.
The devices are a block of a 4x4x8 slice.
Arguments:
- x_seq: bfloat16 [16384, 512], P(('ens', 'sp')), parts along dimension 0
- w_past: bfloat16 [2, 8, 512, 512], replicated
- w_now: bfloat16 [2, 8, 512, 512], replicated
- b_conv: float32 [2, 8, 512], replicated
- w_res: bfloat16 [2, 8, 256, 512], replicated
- w_skip: bfloat16 [2, 8, 256, 256], replicated
- w_out1: bfloat16 [256, 256], replicated
- b_out1: float32 [256], replicated
- w_out2: bfloat16 [256, 256], replicated
- b_out2: float32 [256], replicated
Outputs:
- output 1: float32 [16384, 256], P(('ens', 'sp')), parts along dimension 0
- output 2: bfloat16 [16384, 512], P(('ens', 'sp')), parts along dimension 0
There are 2 independent parts. A program takes and returns all parts, laid end to end along the dimension named above; an argument that names none is the same for every part.
All inputs are finite; a program needn't handle non-finite values.
Results may differ from a plain program's by a relative error of at most 0.0140783.
Values are sent between devices in bfloat16 or wider.
A program may use at most 768 MiB of HBM per device.

v0:
```python
import jax
import jax.numpy as jnp
from jax import lax
from jax.sharding import PartitionSpec as P


def solution(mesh):
    seq_devs = mesh.shape["sp"]
    shift_perm = [(src, src + 1) for src in range(seq_devs - 1)]
    row_spec = P(("ens", "sp"), None)

    def local_stack(x_seq, w_past, w_now, b_conv, w_res, w_skip, w_out1, b_out1, w_out2, b_out2):
        stacks, cycle = w_past.shape[0], w_past.shape[1]
        gate_ch = b_conv.shape[-1] // 2
        hidden = x_seq
        skip_sum = jnp.zeros((x_seq.shape[0], w_skip.shape[-1]), jnp.float32)
        for stack_idx in range(stacks):
            for layer_pos in range(cycle):
                dilation = 2 ** layer_pos
                halo_rows = lax.ppermute(hidden[-dilation:], "sp", perm=shift_perm)
                shifted = jnp.concatenate([halo_rows, hidden[:-dilation]], axis=0)
                pre_act = (jnp.dot(shifted, w_past[stack_idx, layer_pos], preferred_element_type=jnp.float32)
                           + jnp.dot(hidden, w_now[stack_idx, layer_pos], preferred_element_type=jnp.float32)
                           + b_conv[stack_idx, layer_pos])
                gated = (jnp.tanh(pre_act[:, :gate_ch]) * jax.nn.sigmoid(pre_act[:, gate_ch:])).astype(jnp.bfloat16)
                hidden = (hidden.astype(jnp.float32) + jnp.dot(gated, w_res[stack_idx, layer_pos], preferred_element_type=jnp.float32)).astype(jnp.bfloat16)
                skip_sum = skip_sum + jnp.dot(gated, w_skip[stack_idx, layer_pos], preferred_element_type=jnp.float32)
        skip_act = jax.nn.relu(skip_sum).astype(jnp.bfloat16)
        mid_act = jax.nn.relu(jnp.dot(skip_act, w_out1, preferred_element_type=jnp.float32) + b_out1).astype(jnp.bfloat16)
        logits = jnp.dot(mid_act, w_out2, preferred_element_type=jnp.float32) + b_out2
        return (logits, hidden)

    return jax.shard_map(
        local_stack,
        mesh=mesh,
        in_specs=(row_spec, P(), P(), P(), P(), P(), P(), P(), P(), P()),
        out_specs=(row_spec, row_spec),
        check_vma=False,
    )
```

profile of v0, /device:TPU:113, one launch (start us, length us, event | category | flops | bytes accessed | tf_op | source)
XLA Modules:
  0.0 129.4 jit_solution(7062153553711160561)
XLA Ops:
  0.7 0.8 slice.432
  1.5 4.6 %collective-permute-start = (bf16[1,512]{1,0:T(2,128)(2,1)S(1)}, bf16[1,512]{1,0:T(2,128)(2,1)S(1)}, u32[]{:S(2)}, u32[]{:S(2)}) collective-permute-start(bf16[1,512]{1,0:T(2,128)(2,1)S(1)} %slice.432), channel_id=1, source_target_pairs={{0,1},{1,2},{2,3},{3,4},{4,5},{5,6},{6,7},{8,9},{9,10},{10,11},{11... | collective-permute-start | bytes 3080 | tf_op jit(solution)/shard_map/ppermute | solution.py:20
  6.1 2.2 %fusion.177 = f32[1024,512]{1,0:T(8,128)S(1)} fusion(bf16[1024,512]{1,0:T(8,128)(2,1)} %param.10, bf16[2,8,512,512]{3,2,1,0:T(8,128)(2,1)} %param.12), kind=kOutput, calls=%fused_computation.258 | convolution fusion | flops 536870912 | bytes 3670016 | tf_op jit(solution)/shard_map/dot_general | solution.py:23
  8.4 1.9 %add_add_fusion.15 = f32[1024,512]{1,0:T(8,128)S(1)} fusion(f32[1024,512]{1,0:T(8,128)S(1)} %fusion.177, bf16[1023,512]{1,0:T(8,128)(2,1)S(1)} %bitcast.271, bf16[1,512]{1,0:T(2,128)(2,1)S(1)} %collective-permute-done, f32[512]{0:T(512)S(1)} %bitcast.277, bf16[2,8,512,512]{3,2,1,0:T(8,128)(2,1)} %param.11), kind=kOutput, calls=%fused_computation.31 | convolution fusion | flops 540016640 | bytes 5769216 | tf_op jit(solution)/shard_map/dot_general | solution.py:22
  11.2 0.8 copy-done.2
  12.7 2.5 %collective-permute-start.1 = (bf16[2,512]{1,0:T(2,128)(2,1)S(1)}, bf16[2,512]{1,0:T(2,128)(2,1)S(1)}, u32[]{:S(2)}, u32[]{:S(2)}) collective-permute-start(bf16[2,512]{1,0:T(2,128)(2,1)S(1)} %slice.578), channel_id=1, source_target_pairs={{0,1},{1,2},{2,3},{3,4},{4,5},{5,6},{6,7},{8,9},{9,10},{10,11},{11... | collective-permute-start | bytes 6152 | tf_op jit(solution)/shard_map/ppermute | solution.py:20
  16.0 1.9 %add_add_fusion.14 = f32[1024,512]{1,0:T(8,128)S(1)} fusion(f32[1024,512]{1,0:T(8,128)S(1)} %fusion.174, bf16[1022,512]{1,0:T(8,128)(2,1)S(1)} %bitcast.270, bf16[2,512]{1,0:T(2,128)(2,1)S(1)} %collective-permute-done.1, f32[512]{0:T(512)S(1)} %bitcast.276, bf16[2,8,512,512]{3,2,1,0:T(8,128)(2,1)} %param.11), kind=kOutput, calls=%fused_computation.29 | convolution fusion | flops 540016640 | bytes 5769216 | tf_op jit(solution)/shard_map/dot_general | solution.py:22
  19.5 4.4 %collective-permute-start.2 = (bf16[4,512]{1,0:T(4,128)(2,1)S(1)}, bf16[4,512]{1,0:T(4,128)(2,1)S(1)}, u32[]{:S(2)}, u32[]{:S(2)}) collective-permute-start(bf16[4,512]{1,0:T(4,128)(2,1)S(1)} %slice.582), channel_id=1, source_target_pairs={{0,1},{1,2},{2,3},{3,4},{4,5},{5,6},{6,7},{8,9},{9,10},{10,11},{11... | collective-permute-start | bytes 12296 | tf_op jit(solution)/shard_map/ppermute | solution.py:20
  24.6 0.7 add_add_fusion.13
  26.9 4.2 %collective-permute-start.3 = (bf16[8,512]{1,0:T(8,128)(2,1)S(1)}, bf16[8,512]{1,0:T(8,128)(2,1)S(1)}, u32[]{:S(2)}, u32[]{:S(2)}) collective-permute-start(bf16[8,512]{1,0:T(8,128)(2,1)S(1)} %slice.586), channel_id=1, source_target_pairs={{0,1},{1,2},{2,3},{3,4},{4,5},{5,6},{6,7},{8,9},{9,10},{10,11},{11... | collective-permute-start | bytes 24584 | tf_op jit(solution)/shard_map/ppermute | solution.py:20
  34.3 4.2 %collective-permute-start.4 = (bf16[16,512]{1,0:T(8,128)(2,1)S(1)}, bf16[16,512]{1,0:T(8,128)(2,1)S(1)}, u32[]{:S(2)}, u32[]{:S(2)}) collective-permute-start(bf16[16,512]{1,0:T(8,128)(2,1)S(1)} %slice.590), channel_id=1, source_target_pairs={{0,1},{1,2},{2,3},{3,4},{4,5},{5,6},{6,7},{8,9},{9,10},{10,11},{11... | collective-permute-start | bytes 49160 | tf_op jit(solution)/shard_map/ppermute | solution.py:20
  41.6 4.4 %collective-permute-start.5 = (bf16[32,512]{1,0:T(8,128)(2,1)S(1)}, bf16[32,512]{1,0:T(8,128)(2,1)S(1)}, u32[]{:S(2)}, u32[]{:S(2)}) collective-permute-start(bf16[32,512]{1,0:T(8,128)(2,1)S(1)} %slice.594), channel_id=1, source_target_pairs={{0,1},{1,2},{2,3},{3,4},{4,5},{5,6},{6,7},{8,9},{9,10},{10,11},{11... | collective-permute-start | bytes 98312 | tf_op jit(solution)/shard_map/ppermute | solution.py:20
  49.2 4.3 %collective-permute-start.6 = (bf16[64,512]{1,0:T(8,128)(2,1)S(1)}, bf16[64,512]{1,0:T(8,128)(2,1)S(1)}, u32[]{:S(2)}, u32[]{:S(2)}) collective-permute-start(bf16[64,512]{1,0:T(8,128)(2,1)S(1)} %slice.598), channel_id=1, source_target_pairs={{0,1},{1,2},{2,3},{3,4},{4,5},{5,6},{6,7},{8,9},{9,10},{10,11},{11... | collective-permute-start | bytes 196616 | tf_op jit(solution)/shard_map/ppermute | solution.py:20
  53.9 0.9 collective-permute-done.6
  57.1 4.3 %collective-permute-start.7 = (bf16[128,512]{1,0:T(8,128)(2,1)S(1)}, bf16[128,512]{1,0:T(8,128)(2,1)S(1)}, u32[]{:S(2)}, u32[]{:S(2)}) collective-permute-start(bf16[128,512]{1,0:T(8,128)(2,1)S(1)} %slice.602), channel_id=1, source_target_pairs={{0,1},{1,2},{2,3},{3,4},{4,5},{5,6},{6,7},{8,9},{9,10},{10,11},{11... | collective-permute-start | bytes 393224 | tf_op jit(solution)/shard_map/ppermute | solution.py:20
  61.8 1.6 %collective-permute-done.7 = bf16[128,512]{1,0:T(8,128)(2,1)S(1)} collective-permute-done((bf16[128,512]{1,0:T(8,128)(2,1)S(1)}, bf16[128,512]{1,0:T(8,128)(2,1)S(1)}, u32[]{:S(2)}, u32[]{:S(2)}) %collective-permute-start.7) | collective-permute-done | bytes 131104 | tf_op jit(solution)/shard_map/ppermute | solution.py:20
  65.7 4.4 %collective-permute-start.8 = (bf16[1,512]{1,0:T(2,128)(2,1)S(1)}, bf16[1,512]{1,0:T(2,128)(2,1)S(1)}, u32[]{:S(2)}, u32[]{:S(2)}) collective-permute-start(bf16[1,512]{1,0:T(2,128)(2,1)S(1)} %slice.606), channel_id=1, source_target_pairs={{0,1},{1,2},{2,3},{3,4},{4,5},{5,6},{6,7},{8,9},{9,10},{10,11},{11... | collective-permute-start | bytes 3080 | tf_op jit(solution)/shard_map/ppermute | solution.py:20
  70.8 0.7 add_add_fusion.7
  73.1 4.2 %collective-permute-start.9 = (bf16[2,512]{1,0:T(2,128)(2,1)S(1)}, bf16[2,512]{1,0:T(2,128)(2,1)S(1)}, u32[]{:S(2)}, u32[]{:S(2)}) collective-permute-start(bf16[2,512]{1,0:T(2,128)(2,1)S(1)} %slice.610), channel_id=1, source_target_pairs={{0,1},{1,2},{2,3},{3,4},{4,5},{5,6},{6,7},{8,9},{9,10},{10,11},{11... | collective-permute-start | bytes 6152 | tf_op jit(solution)/shard_map/ppermute | solution.py:20
  78.0 0.7 add_add_fusion.6
  80.4 4.2 %collective-permute-start.10 = (bf16[4,512]{1,0:T(4,128)(2,1)S(1)}, bf16[4,512]{1,0:T(4,128)(2,1)S(1)}, u32[]{:S(2)}, u32[]{:S(2)}) collective-permute-start(bf16[4,512]{1,0:T(4,128)(2,1)S(1)} %slice.614), channel_id=1, source_target_pairs={{0,1},{1,2},{2,3},{3,4},{4,5},{5,6},{6,7},{8,9},{9,10},{10,11},{11... | collective-permute-start | bytes 12296 | tf_op jit(solution)/shard_map/ppermute | solution.py:20
  85.3 0.7 add_add_fusion.5
  87.6 4.4 %collective-permute-start.11 = (bf16[8,512]{1,0:T(8,128)(2,1)S(1)}, bf16[8,512]{1,0:T(8,128)(2,1)S(1)}, u32[]{:S(2)}, u32[]{:S(2)}) collective-permute-start(bf16[8,512]{1,0:T(8,128)(2,1)S(1)} %slice.618), channel_id=1, source_target_pairs={{0,1},{1,2},{2,3},{3,4},{4,5},{5,6},{6,7},{8,9},{9,10},{10,11},{11... | collective-permute-start | bytes 24584 | tf_op jit(solution)/shard_map/ppermute | solution.py:20
  95.0 4.2 %collective-permute-start.12 = (bf16[16,512]{1,0:T(8,128)(2,1)S(1)}, bf16[16,512]{1,0:T(8,128)(2,1)S(1)}, u32[]{:S(2)}, u32[]{:S(2)}) collective-permute-start(bf16[16,512]{1,0:T(8,128)(2,1)S(1)} %slice.622), channel_id=1, source_target_pairs={{0,1},{1,2},{2,3},{3,4},{4,5},{5,6},{6,7},{8,9},{9,10},{10,11},{11... | collective-permute-start | bytes 49160 | tf_op jit(solution)/shard_map/ppermute | solution.py:20
  102.3 4.2 %collective-permute-start.13 = (bf16[32,512]{1,0:T(8,128)(2,1)S(1)}, bf16[32,512]{1,0:T(8,128)(2,1)S(1)}, u32[]{:S(2)}, u32[]{:S(2)}) collective-permute-start(bf16[32,512]{1,0:T(8,128)(2,1)S(1)} %slice.626), channel_id=1, source_target_pairs={{0,1},{1,2},{2,3},{3,4},{4,5},{5,6},{6,7},{8,9},{9,10},{10,11},{11... | collective-permute-start | bytes 98312 | tf_op jit(solution)/shard_map/ppermute | solution.py:20
  109.9 4.3 %collective-permute-start.14 = (bf16[64,512]{1,0:T(8,128)(2,1)S(1)}, bf16[64,512]{1,0:T(8,128)(2,1)S(1)}, u32[]{:S(2)}, u32[]{:S(2)}) collective-permute-start(bf16[64,512]{1,0:T(8,128)(2,1)S(1)} %slice.630), channel_id=1, source_target_pairs={{0,1},{1,2},{2,3},{3,4},{4,5},{5,6},{6,7},{8,9},{9,10},{10,11},{11... | collective-permute-start | bytes 196616 | tf_op jit(solution)/shard_map/ppermute | solution.py:20
  114.6 0.9 collective-permute-done.14
  117.8 4.3 %collective-permute-start.15 = (bf16[128,512]{1,0:T(8,128)(2,1)S(1)}, bf16[128,512]{1,0:T(8,128)(2,1)S(1)}, u32[]{:S(2)}, u32[]{:S(2)}) collective-permute-start(bf16[128,512]{1,0:T(8,128)(2,1)S(1)} %slice.634), channel_id=1, source_target_pairs={{0,1},{1,2},{2,3},{3,4},{4,5},{5,6},{6,7},{8,9},{9,10},{10,11},{11... | collective-permute-start | bytes 393224 | tf_op jit(solution)/shard_map/ppermute | solution.py:20
  122.5 1.6 %collective-permute-done.15 = bf16[128,512]{1,0:T(8,128)(2,1)S(1)} collective-permute-done((bf16[128,512]{1,0:T(8,128)(2,1)S(1)}, bf16[128,512]{1,0:T(8,128)(2,1)S(1)}, u32[]{:S(2)}, u32[]{:S(2)}) %collective-permute-start.15) | collective-permute-done | bytes 131104 | tf_op jit(solution)/shard_map/ppermute | solution.py:20
  125.2 1.4 %add_convert_fusion = bf16[1024,512]{1,0:T(8,128)(2,1)} fusion(bf16[1024,512]{1,0:T(8,128)(2,1)S(1)} %add_convert_fusion.1, bf16[1024,256]{1,0:T(8,128)(2,1)S(1)} %fusion.131, bf16[2,8,256,512]{3,2,1,0:T(8,128)(2,1)S(1)} %copy-done.3), kind=kOutput, calls=%fused_computation | convolution fusion | flops 270008320 | bytes 2883584 | tf_op jit(solution)/shard_map/dot_general | solution.py:26
  126.7 1.4 %fusion.3 = bf16[1024,256]{1,0:T(8,128)(2,1)S(1)} fusion(bf16[256,256]{1,0:T(8,128)(2,1)S(1)} %copy-done, f32[1024,256]{1,0:T(8,128)S(1)} %convolution_add_fusion.3, bf16[1024,256]{1,0:T(8,128)(2,1)S(1)} %fusion.131, f32[256]{0:T(256)S(1)} %copy-done.7, bf16[2,8,256,256]{3,2,1,0:T(8,128)(2,1)} %param.15), kind=kOutput, calls=%fused_computation.52 | convolution fusion | flops 270008320 | bytes 2360320 | tf_op jit(solution)/shard_map/dot_general | solution.py:29
  128.1 1.3 convolution_add_fusion
  (131 shorter events, 41.1 us)
Async XLA Ops:
  0.6 126.0 %copy-start = (bf16[256,256]{1,0:T(8,128)(2,1)S(1)}, bf16[256,256]{1,0:T(8,128)(2,1)}, u32[]{:S(2)}) copy-start(bf16[256,256]{1,0:T(8,128)(2,1)} %param.16) | copy-start | bytes 393220
  0.6 7.7 %copy-start.1 = (bf16[1024,512]{1,0:T(8,128)(2,1)S(1)}, bf16[1024,512]{1,0:T(8,128)(2,1)}, u32[]{:S(2)}) copy-start(bf16[1024,512]{1,0:T(8,128)(2,1)} %param.10) | copy-start | bytes 3145732
  0.7 7.6 %copy-start.6 = (f32[2,8,512]{2,1,0:T(8,128)S(1)}, f32[2,8,512]{2,1,0:T(8,128)}, u32[]{:S(2)}) copy-start(f32[2,8,512]{2,1,0:T(8,128)} %param.13) | copy-start | bytes 98308
  1.5 6.9 %collective-permute-start = (bf16[1,512]{1,0:T(2,128)(2,1)S(1)}, bf16[1,512]{1,0:T(2,128)(2,1)S(1)}, u32[]{:S(2)}, u32[]{:S(2)}) collective-permute-start(bf16[1,512]{1,0:T(2,128)(2,1)S(1)} %slice.432), channel_id=1, source_target_pairs={{0,1},{1,2},{2,3},{3,4},{4,5},{5,6},{6,7},{8,9},{9,10},{10,11},{11... | collective-permute-start | bytes 3080 | tf_op jit(solution)/shard_map/ppermute | solution.py:20
  6.1 4.7 %copy-start.3 = (bf16[2,8,256,512]{3,2,1,0:T(8,128)(2,1)S(1)}, bf16[2,8,256,512]{3,2,1,0:T(8,128)(2,1)}, u32[]{:S(2)}) copy-start(bf16[2,8,256,512]{3,2,1,0:T(8,128)(2,1)} %param.14) | copy-start | bytes 12582916
  8.4 3.6 %copy-start.2 = (bf16[2,8,512,512]{3,2,1,0:T(8,128)(2,1)S(1)}, bf16[2,8,512,512]{3,2,1,0:T(8,128)(2,1)}, u32[]{:S(2)}) copy-start(bf16[2,8,512,512]{3,2,1,0:T(8,128)(2,1)} %param.12) | copy-start | bytes 25165828
  11.2 4.1 %copy-start.4 = (bf16[2,8,256,256]{3,2,1,0:T(8,128)(2,1)S(1)}, bf16[2,8,256,256]{3,2,1,0:T(8,128)(2,1)}, u32[]{:S(2)}) copy-start(bf16[2,8,256,256]{3,2,1,0:T(8,128)(2,1)} %param.15) | copy-start | bytes 6291460
  12.7 3.3 %collective-permute-start.1 = (bf16[2,512]{1,0:T(2,128)(2,1)S(1)}, bf16[2,512]{1,0:T(2,128)(2,1)S(1)}, u32[]{:S(2)}, u32[]{:S(2)}) collective-permute-start(bf16[2,512]{1,0:T(2,128)(2,1)S(1)} %slice.578), channel_id=1, source_target_pairs={{0,1},{1,2},{2,3},{3,4},{4,5},{5,6},{6,7},{8,9},{9,10},{10,11},{11... | collective-permute-start | bytes 6152 | tf_op jit(solution)/shard_map/ppermute | solution.py:20
  16.0 8.6 %slice-start = ((s8[8388608]{0:T(1024)(128)(4,1)}), s8[4194304]{0:T(1024)(128)(4,1)S(1)}, s32[]{:S(2)}) async-start(s8[8388608]{0:T(1024)(128)(4,1)} %bitcast.272), calls=%async_computation | async-start | bytes 8388608
  18.3 6.3 %slice-start.1 = ((s8[8388608]{0:T(1024)(128)(4,1)}), s8[4194304]{0:T(1024)(128)(4,1)S(1)}, s32[]{:S(2)}) async-start(s8[8388608]{0:T(1024)(128)(4,1)} %bitcast.272), calls=%async_computation.1 | async-start | bytes 8388608
  19.5 5.1 %collective-permute-start.2 = (bf16[4,512]{1,0:T(4,128)(2,1)S(1)}, bf16[4,512]{1,0:T(4,128)(2,1)S(1)}, u32[]{:S(2)}, u32[]{:S(2)}) collective-permute-start(bf16[4,512]{1,0:T(4,128)(2,1)S(1)} %slice.582), channel_id=1, source_target_pairs={{0,1},{1,2},{2,3},{3,4},{4,5},{5,6},{6,7},{8,9},{9,10},{10,11},{11... | collective-permute-start | bytes 12296 | tf_op jit(solution)/shard_map/ppermute | solution.py:20
  26.9 5.0 %collective-permute-start.3 = (bf16[8,512]{1,0:T(8,128)(2,1)S(1)}, bf16[8,512]{1,0:T(8,128)(2,1)S(1)}, u32[]{:S(2)}, u32[]{:S(2)}) collective-permute-start(bf16[8,512]{1,0:T(8,128)(2,1)S(1)} %slice.586), channel_id=1, source_target_pairs={{0,1},{1,2},{2,3},{3,4},{4,5},{5,6},{6,7},{8,9},{9,10},{10,11},{11... | collective-permute-start | bytes 24584 | tf_op jit(solution)/shard_map/ppermute | solution.py:20
  34.3 5.1 %collective-permute-start.4 = (bf16[16,512]{1,0:T(8,128)(2,1)S(1)}, bf16[16,512]{1,0:T(8,128)(2,1)S(1)}, u32[]{:S(2)}, u32[]{:S(2)}) collective-permute-start(bf16[16,512]{1,0:T(8,128)(2,1)S(1)} %slice.590), channel_id=1, source_target_pairs={{0,1},{1,2},{2,3},{3,4},{4,5},{5,6},{6,7},{8,9},{9,10},{10,11},{11... | collective-permute-start | bytes 49160 | tf_op jit(solution)/shard_map/ppermute | solution.py:20
  41.6 5.2 %collective-permute-start.5 = (bf16[32,512]{1,0:T(8,128)(2,1)S(1)}, bf16[32,512]{1,0:T(8,128)(2,1)S(1)}, u32[]{:S(2)}, u32[]{:S(2)}) collective-permute-start(bf16[32,512]{1,0:T(8,128)(2,1)S(1)} %slice.594), channel_id=1, source_target_pairs={{0,1},{1,2},{2,3},{3,4},{4,5},{5,6},{6,7},{8,9},{9,10},{10,11},{11... | collective-permute-start | bytes 98312 | tf_op jit(solution)/shard_map/ppermute | solution.py:20
  49.2 5.6 %collective-permute-start.6 = (bf16[64,512]{1,0:T(8,128)(2,1)S(1)}, bf16[64,512]{1,0:T(8,128)(2,1)S(1)}, u32[]{:S(2)}, u32[]{:S(2)}) collective-permute-start(bf16[64,512]{1,0:T(8,128)(2,1)S(1)} %slice.598), channel_id=1, source_target_pairs={{0,1},{1,2},{2,3},{3,4},{4,5},{5,6},{6,7},{8,9},{9,10},{10,11},{11... | collective-permute-start | bytes 196616 | tf_op jit(solution)/shard_map/ppermute | solution.py:20
  57.1 6.2 %collective-permute-start.7 = (bf16[128,512]{1,0:T(8,128)(2,1)S(1)}, bf16[128,512]{1,0:T(8,128)(2,1)S(1)}, u32[]{:S(2)}, u32[]{:S(2)}) collective-permute-start(bf16[128,512]{1,0:T(8,128)(2,1)S(1)} %slice.602), channel_id=1, source_target_pairs={{0,1},{1,2},{2,3},{3,4},{4,5},{5,6},{6,7},{8,9},{9,10},{10,11},{11... | collective-permute-start | bytes 393224 | tf_op jit(solution)/shard_map/ppermute | solution.py:20
  65.7 5.1 %collective-permute-start.8 = (bf16[1,512]{1,0:T(2,128)(2,1)S(1)}, bf16[1,512]{1,0:T(2,128)(2,1)S(1)}, u32[]{:S(2)}, u32[]{:S(2)}) collective-permute-start(bf16[1,512]{1,0:T(2,128)(2,1)S(1)} %slice.606), channel_id=1, source_target_pairs={{0,1},{1,2},{2,3},{3,4},{4,5},{5,6},{6,7},{8,9},{9,10},{10,11},{11... | collective-permute-start | bytes 3080 | tf_op jit(solution)/shard_map/ppermute | solution.py:20
  73.1 4.9 %collective-permute-start.9 = (bf16[2,512]{1,0:T(2,128)(2,1)S(1)}, bf16[2,512]{1,0:T(2,128)(2,1)S(1)}, u32[]{:S(2)}, u32[]{:S(2)}) collective-permute-start(bf16[2,512]{1,0:T(2,128)(2,1)S(1)} %slice.610), channel_id=1, source_target_pairs={{0,1},{1,2},{2,3},{3,4},{4,5},{5,6},{6,7},{8,9},{9,10},{10,11},{11... | collective-permute-start | bytes 6152 | tf_op jit(solution)/shard_map/ppermute | solution.py:20
  80.4 5.0 %collective-permute-start.10 = (bf16[4,512]{1,0:T(4,128)(2,1)S(1)}, bf16[4,512]{1,0:T(4,128)(2,1)S(1)}, u32[]{:S(2)}, u32[]{:S(2)}) collective-permute-start(bf16[4,512]{1,0:T(4,128)(2,1)S(1)} %slice.614), channel_id=1, source_target_pairs={{0,1},{1,2},{2,3},{3,4},{4,5},{5,6},{6,7},{8,9},{9,10},{10,11},{11... | collective-permute-start | bytes 12296 | tf_op jit(solution)/shard_map/ppermute | solution.py:20
  87.6 5.0 %collective-permute-start.11 = (bf16[8,512]{1,0:T(8,128)(2,1)S(1)}, bf16[8,512]{1,0:T(8,128)(2,1)S(1)}, u32[]{:S(2)}, u32[]{:S(2)}) collective-permute-start(bf16[8,512]{1,0:T(8,128)(2,1)S(1)} %slice.618), channel_id=1, source_target_pairs={{0,1},{1,2},{2,3},{3,4},{4,5},{5,6},{6,7},{8,9},{9,10},{10,11},{11... | collective-permute-start | bytes 24584 | tf_op jit(solution)/shard_map/ppermute | solution.py:20
  95.0 5.1 %collective-permute-start.12 = (bf16[16,512]{1,0:T(8,128)(2,1)S(1)}, bf16[16,512]{1,0:T(8,128)(2,1)S(1)}, u32[]{:S(2)}, u32[]{:S(2)}) collective-permute-start(bf16[16,512]{1,0:T(8,128)(2,1)S(1)} %slice.622), channel_id=1, source_target_pairs={{0,1},{1,2},{2,3},{3,4},{4,5},{5,6},{6,7},{8,9},{9,10},{10,11},{11... | collective-permute-start | bytes 49160 | tf_op jit(solution)/shard_map/ppermute | solution.py:20
  102.3 5.2 %collective-permute-start.13 = (bf16[32,512]{1,0:T(8,128)(2,1)S(1)}, bf16[32,512]{1,0:T(8,128)(2,1)S(1)}, u32[]{:S(2)}, u32[]{:S(2)}) collective-permute-start(bf16[32,512]{1,0:T(8,128)(2,1)S(1)} %slice.626), channel_id=1, source_target_pairs={{0,1},{1,2},{2,3},{3,4},{4,5},{5,6},{6,7},{8,9},{9,10},{10,11},{11... | collective-permute-start | bytes 98312 | tf_op jit(solution)/shard_map/ppermute | solution.py:20
  109.9 5.6 %collective-permute-start.14 = (bf16[64,512]{1,0:T(8,128)(2,1)S(1)}, bf16[64,512]{1,0:T(8,128)(2,1)S(1)}, u32[]{:S(2)}, u32[]{:S(2)}) collective-permute-start(bf16[64,512]{1,0:T(8,128)(2,1)S(1)} %slice.630), channel_id=1, source_target_pairs={{0,1},{1,2},{2,3},{3,4},{4,5},{5,6},{6,7},{8,9},{9,10},{10,11},{11... | collective-permute-start | bytes 196616 | tf_op jit(solution)/shard_map/ppermute | solution.py:20
  117.8 6.2 %collective-permute-start.15 = (bf16[128,512]{1,0:T(8,128)(2,1)S(1)}, bf16[128,512]{1,0:T(8,128)(2,1)S(1)}, u32[]{:S(2)}, u32[]{:S(2)}) collective-permute-start(bf16[128,512]{1,0:T(8,128)(2,1)S(1)} %slice.634), channel_id=1, source_target_pairs={{0,1},{1,2},{2,3},{3,4},{4,5},{5,6},{6,7},{8,9},{9,10},{10,11},{11... | collective-permute-start | bytes 393224 | tf_op jit(solution)/shard_map/ppermute | solution.py:20
  124.8 1.9 %copy-start.7 = (f32[256]{0:T(256)S(1)}, f32[256]{0:T(256)}, u32[]{:S(2)}) copy-start(f32[256]{0:T(256)} %param.17) | copy-start | bytes 3076
  125.2 2.9 %copy-start.5 = (bf16[256,256]{1,0:T(8,128)(2,1)S(1)}, bf16[256,256]{1,0:T(8,128)(2,1)}, u32[]{:S(2)}) copy-start(bf16[256,256]{1,0:T(8,128)(2,1)} %param.18) | copy-start | bytes 393220
  125.2 2.9 %copy-start.8 = (f32[256]{0:T(256)S(1)}, f32[256]{0:T(256)}, u32[]{:S(2)}) copy-start(f32[256]{0:T(256)} %param.19) | copy-start | bytes 3076
where the time goes:
time: 130 us; the launch traced here: 129 us
  starting transfers between devices  67.1 us (52%)
  matrix products  41.6 us (32%)
  waiting for transfers between devices  9.67 us (7%)
  other arithmetic  7.07 us (5%)
  local copies, waits for them, and re-layouts  2.43 us (2%)
  between operations  1.51 us (1%)
    ppermute x16, starting transfers between devices, local_stack(): halo_rows = lax.ppermute(hidden[-dilation:], 'sp', perm=shift_perm)  67.1 us
    dot_general x16, matrix products, local_stack(): jnp.dot(shifted, w_past[stack_idx, layer_pos], preferred_element_type=jnp...  13.7 us
    dot_general x16, matrix products, local_stack(): jnp.dot(hidden, w_now[stack_idx, layer_pos], preferred_element_type=jnp.f...  12.7 us
    ppermute x16, waiting for transfers between devices, local_stack(): halo_rows = lax.ppermute(hidden[-dilation:], 'sp', perm=shift_perm)  9.67 us
    dot_general x16, matrix products, local_stack(): jnp.dot(gated, w_res[stack_idx, layer_pos], preferred_element_type=jnp.fl...  8.03 us
    convert_element_type x16, other arithmetic, local_stack(): (jnp.tanh(pre_act[:, :gate_ch]) * jax.nn.sigmoid(pre_act[:, gate_ch:])).a...  7.07 us
    dot_general x15, matrix products, local_stack(): jnp.dot(gated, w_skip[stack_idx, layer_pos], preferred_element_type=jnp.f...  4.41 us
  transfers between devices with their start and end apart: 16, of which 15 were waited for; matrix products, arithmetic and copies ran while one was open for 6% of the time, Pallas kernels for 0%

commit v1 on v0

v1 whole, which is shorter than its diff:
```python
import functools

import jax
import jax.numpy as jnp
from jax import lax
from jax.experimental import pallas as pl
from jax.experimental.pallas import tpu as pltpu
from jax.sharding import PartitionSpec as P

TILE = 256
PAD = 128
MESH = pl.DeviceIdType.MESH


def order_of(layers, tiles, lag):
    keyed = []
    for layer in range(layers):
        for tile in range(tiles):
            back = tiles - 1 - tile
            keyed.append((tiles * layer + back * (1 + lag), layer, tile))
    return [(layer, tile) for _, layer, tile in sorted(keyed)]


def kernel(n, stacks, cycle, x_hbm, wp_hbm, wn_hbm, b_hbm, wr_hbm, ws_hbm, w1_hbm, c1_hbm, w2_hbm, c2_hbm,
           y_hbm, hout_hbm,
           h, skip, y, wz, wrs, b, w1, c1, w2, c2, halo,
           x_sem, w_sem, small_sem, send_sem, recv_sem, y_sem, h_sem):
    rows, res = x_hbm.shape
    gate = wr_hbm.shape[2]
    layers = stacks * cycle
    tiles = rows // TILE
    me = lax.axis_index("sp")
    right = lax.rem(me + 1, n)
    left = lax.rem(me + n - 1, n)
    ens = lax.axis_index("ens")

    barrier = pltpu.get_barrier_semaphore()
    pl.semaphore_signal(barrier, inc=1, device_id=(ens, left), device_id_type=MESH)

    def dilation(layer):
        return 2 ** (layer % cycle)

    def halo_rows(layer):
        return max(16, dilation(layer))

    x_copies = []
    for tile in range(tiles):
        x_copies.append(pltpu.make_async_copy(
            x_hbm.at[pl.ds(tile * TILE, TILE)], h.at[pl.ds(PAD + tile * TILE, TILE)], x_sem.at[tile]))
    w_copies = []
    for layer in range(layers):
        s, k = layer // cycle, layer % cycle
        w_copies.append([
            pltpu.make_async_copy(wp_hbm.at[s, k], wz.at[layer, pl.ds(0, res)], w_sem.at[layer]),
            pltpu.make_async_copy(wn_hbm.at[s, k], wz.at[layer, pl.ds(res, res)], w_sem.at[layer]),
            pltpu.make_async_copy(wr_hbm.at[s, k], wrs.at[layer, :, pl.ds(0, res)], w_sem.at[layer]),
            pltpu.make_async_copy(ws_hbm.at[s, k], wrs.at[layer, :, pl.ds(res, gate)], w_sem.at[layer]),
        ])
    small_copies = [
        pltpu.make_async_copy(b_hbm, b, small_sem.at[0]),
        pltpu.make_async_copy(w1_hbm, w1, small_sem.at[1]),
        pltpu.make_async_copy(c1_hbm, c1, small_sem.at[2]),
        pltpu.make_async_copy(w2_hbm, w2, small_sem.at[3]),
        pltpu.make_async_copy(c2_hbm, c2, small_sem.at[4]),
    ]
    x_copies[-1].start()
    small_copies[0].start()
    for c in w_copies[0]:
        c.start()
    for c in reversed(x_copies[:-1]):
        c.start()
    for layer in range(1, layers):
        for c in w_copies[layer]:
            c.start()
    for c in small_copies[1:]:
        c.start()

    def halo_send(layer):
        r = halo_rows(layer)
        return pltpu.make_async_remote_copy(
            src_ref=h.at[pl.ds(PAD + rows - r, r)],
            dst_ref=halo.at[layer, pl.ds(PAD - r, r)],
            send_sem=send_sem.at[layer], recv_sem=recv_sem.at[layer],
            device_id=(ens, right), device_id_type=MESH)

    def past_rows(tile, d):
        base = PAD + tile * TILE
        if d % 16 == 0:
            return h[pl.ds(base - d, TILE), :]
        wide = h[pl.ds(base - 16, TILE + 16), :].astype(jnp.float32)
        return wide[16 - d:16 - d + TILE].astype(jnp.bfloat16)

    pl.semaphore_wait(barrier, 1)

    x_ready, w_ready = set(), set()
    last_tile = tiles - 1

    def need_x(tile):
        if tile >= 0 and tile not in x_ready:
            x_ready.add(tile)
            x_copies[tile].wait()
            if tile == last_tile:
                halo_send(0).start()

    def need_w(layer):
        if layer not in w_ready:
            w_ready.add(layer)
            for c in w_copies[layer]:
                c.wait()

    small_ready = False
    for layer, tile in order_of(layers, tiles, 1):
        d = dilation(layer)
        if layer == 0:
            need_x(tile)
            need_x(tile - 1)
            if not small_ready:
                small_ready = True
                small_copies[0].wait()
        need_w(layer)
        if tile == 0:
            r = halo_rows(layer)
            halo_send(layer).wait_recv()
            got = halo[layer, pl.ds(PAD - r, r), :]
            h[pl.ds(PAD - r, r), :] = jnp.where(me > 0, got, jnp.zeros_like(got))
        mine = pl.ds(PAD + tile * TILE, TILE)
        now = h[mine, :]
        z = jnp.dot(jnp.concatenate([past_rows(tile, d), now], axis=1), wz[layer],
                    preferred_element_type=jnp.float32)
        s, k = layer // cycle, layer % cycle
        z = z + b[s, pl.ds(k, 1), :]
        g = (jnp.tanh(z[:, :gate]) * (0.5 * jnp.tanh(0.5 * z[:, gate:]) + 0.5)).astype(jnp.bfloat16)
        o = jnp.dot(g, wrs[layer], preferred_element_type=jnp.float32)
        if layer > 0 and tile == last_tile:
            halo_send(layer).wait_send()
        if layer == 0 and tile == last_tile:
            halo_send(0).wait_send()
        h[mine, :] = (now.astype(jnp.float32) + o[:, :res]).astype(jnp.bfloat16)
        rows_here = pl.ds(tile * TILE, TILE)
        if layer == 0:
            skip[rows_here, :] = o[:, res:]
        else:
            skip[rows_here, :] = skip[rows_here, :] + o[:, res:]
        if layer + 1 < layers and tile == last_tile:
            halo_send(layer + 1).start()
        if layer + 1 == layers:
            pltpu.make_async_copy(h.at[mine], hout_hbm.at[rows_here], h_sem.at[tile]).start()
            if tile == last_tile:
                for c in small_copies[1:]:
                    c.wait()
            a = jnp.maximum(skip[rows_here, :], 0.0).astype(jnp.bfloat16)
            m = jnp.dot(a, w1[...], preferred_element_type=jnp.float32) + c1[...]
            m = jnp.maximum(m, 0.0).astype(jnp.bfloat16)
            y[rows_here, :] = jnp.dot(m, w2[...], preferred_element_type=jnp.float32) + c2[...]
            pltpu.make_async_copy(y.at[rows_here], y_hbm.at[rows_here], y_sem.at[tile]).start()
    for tile in range(tiles):
        rows_here = pl.ds(tile * TILE, TILE)
        pltpu.make_async_copy(h.at[pl.ds(PAD + tile * TILE, TILE)], hout_hbm.at[rows_here], h_sem.at[tile]).wait()
        pltpu.make_async_copy(y.at[rows_here], y_hbm.at[rows_here], y_sem.at[tile]).wait()


def solution(mesh):
    n = mesh.shape["sp"]
    row_spec = P(("ens", "sp"), None)

    def local_stack(x_seq, w_past, w_now, b_conv, w_res, w_skip, w_out1, b_out1, w_out2, b_out2):
        stacks, cycle, res, _ = w_past.shape
        gate = b_conv.shape[-1] // 2
        skip_ch = w_skip.shape[-1]
        classes = w_out2.shape[-1]
        rows = x_seq.shape[0]
        layers = stacks * cycle
        tiles = rows // TILE
        any_spec = pl.BlockSpec(memory_space=pl.ANY)
        return pl.pallas_call(
            functools.partial(kernel, n, stacks, cycle),
            out_shape=(jax.ShapeDtypeStruct((rows, classes), jnp.float32),
                       jax.ShapeDtypeStruct((rows, res), jnp.bfloat16)),
            in_specs=[any_spec] * 10,
            out_specs=(any_spec, any_spec),
            scratch_shapes=[
                pltpu.VMEM((PAD + rows, res), jnp.bfloat16),
                pltpu.VMEM((rows, skip_ch), jnp.float32),
                pltpu.VMEM((rows, classes), jnp.float32),
                pltpu.VMEM((layers, 2 * res, 2 * gate), jnp.bfloat16),
                pltpu.VMEM((layers, gate, res + skip_ch), jnp.bfloat16),
                pltpu.VMEM(b_conv.shape, jnp.float32),
                pltpu.VMEM(w_out1.shape, jnp.bfloat16),
                pltpu.VMEM((1, skip_ch), jnp.float32),
                pltpu.VMEM(w_out2.shape, jnp.bfloat16),
                pltpu.VMEM((1, classes), jnp.float32),
                pltpu.VMEM((layers, PAD, res), jnp.bfloat16),
                pltpu.SemaphoreType.DMA((tiles,)),
                pltpu.SemaphoreType.DMA((layers,)),
                pltpu.SemaphoreType.DMA((5,)),
                pltpu.SemaphoreType.DMA((layers,)),
                pltpu.SemaphoreType.DMA((layers,)),
                pltpu.SemaphoreType.DMA((tiles,)),
                pltpu.SemaphoreType.DMA((tiles,)),
            ],
            compiler_params=pltpu.CompilerParams(
                collective_id=0, has_side_effects=True, vmem_limit_bytes=60 * 1024 * 1024),
            name="stack",
        )(x_seq, w_past, w_now, b_conv, w_res, w_skip, w_out1, b_out1.reshape(1, -1), w_out2, b_out2.reshape(1, -1))

    return jax.shard_map(
        local_stack,
        mesh=mesh,
        in_specs=(row_spec, P(), P(), P(), P(), P(), P(), P(), P(), P()),
        out_specs=(row_spec, row_spec),
        check_vma=False,
    )
```

time: 130 us -> 54.4 us (0.42)
  the two profiles are of different devices: /device:TPU:113 before, /device:TPU:112 now
where the time goes in v1:
time: 54.4 us; the launch traced here: 54.3 us
  Pallas kernels  49.1 us (90%)
  local copies, waits for them, and re-layouts  4.52 us (8%)
  between operations  0.64 us (1%)
    pallas_call x1, Pallas kernels, local_stack(): pl.pallas_call(functools.partial(kernel, n, stacks, cycle), out_shape=(ja...  49.1 us
    unnamed x2, local copies, waits for them, and re-layouts  4.52 us

profile of v1, /device:TPU:112, one launch (start us, length us, event | category | flops | bytes accessed | tf_op | source)
XLA Modules:
  0.0 54.3 jit_solution(4579931580707153743)
XLA Ops:
  0.6 49.1 %stack.1 = (f32[1024,256]{1,0:T(8,128)}, bf16[1024,512]{1,0:T(8,128)(2,1)}) custom-call(bf16[1024,512]{1,0:T(8,128)(2,1)} %x_hbm.1, bf16[2,8,512,512]{3,2,1,0:T(8,128)(2,1)} %wp_hbm.1, bf16[2,8,512,512]{3,2,1,0:T(8,128)(2,1)} %wn_hbm.1, f32[2,8,512]{2,1,0:T(8,128)} %b_hbm.1, bf16[2,8,256,512]{3,2,1,0:T(8,128)(2,1)} %wr_hbm.1, ...), custom_call_target="tpu_custom_call" | custom-call | tf_op jit(solution)/shard_map/stack/pallas_call | solution.py:175
  49.8 2.3 %copy.14 = f32[1024,256]{1,0:T(8,128)} copy(f32[1024,256]{1,0:T(8,128)} %get-tuple-element.4) | data formatting | bytes 2097152
  52.0 2.3 %copy.15 = bf16[1024,512]{1,0:T(8,128)(2,1)} copy(bf16[1024,512]{1,0:T(8,128)(2,1)} %get-tuple-element.5) | data formatting | bytes 2097152

commit v2 on v0

v2 whole, which is shorter than its diff:
```python
import functools

import jax
import jax.numpy as jnp
from jax import lax
from jax.experimental import pallas as pl
from jax.experimental.pallas import tpu as pltpu
from jax.sharding import PartitionSpec as P

TILE = 256
PIECE = 64
PAD = 128
SIDE = 256
BUFFERS = 4
LAGS = (5, 3, 2, 0)
MESH = pl.DeviceIdType.MESH
F32 = jnp.float32
BF16 = jnp.bfloat16


def program_of(layers, tiles, cycle):
    steps = sorted((tiles * layer + LAGS[tile], layer, tile) for layer in range(layers) for tile in range(tiles))
    items = [("z", layer, tile) for _, layer, tile in steps]
    hi, lo = (tiles - 1, tiles - 2), (tiles - 3, tiles - 4)
    half, end = cycle - 2, layers - 1
    at = items.index(("z", cycle - 2, 0))
    items.insert(at, ("s", lo, 0, half, False))
    items.insert(at - 1, ("s", hi, 0, half, False))
    at = items.index(("z", layers - 1, 0))
    items.insert(at, ("s", hi, half, end, False))
    items += [("s", hi, end, layers, True)]
    at = items.index(("z", layers - 1, 0))
    items.insert(at, ("s", lo, half, end, False))
    items += [("s", lo, end, layers, True)]
    return items


def group_bounds(layers, cycle):
    cuts = [0, 1, 3] + list(range(cycle, layers + 1, cycle))
    return list(zip(cuts[:-1], cuts[1:]))


def kernel(n, stacks, cycle, x_hbm, wp_hbm, wn_hbm, b_hbm, wr_hbm, ws_hbm, w1_hbm, c1_hbm, w2_hbm, c2_hbm,
           y, hout, h, skip, g_all, wz, wr, ws, b, w1, c1, w2, c2, halo, out_rows,
           x_sem, w_sem, small_sem, send_sem, recv_sem):
    rows, res = x_hbm.shape
    gate = wr_hbm.shape[2]
    layers = stacks * cycle
    tiles = rows // TILE
    me = lax.axis_index("sp")
    ens = lax.axis_index("ens")
    first, last = me == 0, me == n - 1

    barrier = pltpu.get_barrier_semaphore()

    @pl.when(jnp.logical_not(first))
    def _():
        pl.semaphore_signal(barrier, inc=1, device_id=(ens, me - 1), device_id_type=MESH)

    def where_of(layer):
        return layer // cycle, layer % cycle

    def dilation(layer):
        return 2 ** (layer % cycle)

    def halo_rows(layer):
        return max(16, dilation(layer))

    x_copies = [pltpu.make_async_copy(
        x_hbm.at[pl.ds(tile * TILE, TILE)], h.at[pl.ds(PAD + tile * TILE, TILE)], x_sem.at[tile])
        for tile in range(tiles)]
    groups = group_bounds(layers, cycle)
    group_of = {layer: i for i, (lo, hi) in enumerate(groups) for layer in range(lo, hi)}
    w_copies = []
    for i, (lo, hi) in enumerate(groups):
        s, k = where_of(lo)
        span = pl.ds(k, hi - lo)
        sem = w_sem.at[i]
        w_copies.append([
            pltpu.make_async_copy(wp_hbm.at[s, span], wz.at[pl.ds(lo, hi - lo), pl.ds(0, res)], sem),
            pltpu.make_async_copy(wn_hbm.at[s, span], wz.at[pl.ds(lo, hi - lo), pl.ds(res, res)], sem),
            pltpu.make_async_copy(wr_hbm.at[s, span], wr.at[pl.ds(lo, hi - lo)], sem),
            pltpu.make_async_copy(ws_hbm.at[s, span], ws.at[pl.ds(lo, hi - lo)], sem)])
    small_copies = [pltpu.make_async_copy(src, dst, small_sem.at[i]) for i, (src, dst) in enumerate(
        ((b_hbm, b), (w1_hbm, w1), (c1_hbm, c1), (w2_hbm, w2), (c2_hbm, c2)))]
    x_copies[-1].start()
    small_copies[0].start()
    for c in w_copies[0]:
        c.start()
    for c in reversed(x_copies[:-1]):
        c.start()
    for c in small_copies[1:]:
        c.start()

    def halo_send(layer, src):
        r = halo_rows(layer)
        return pltpu.make_async_remote_copy(
            src_ref=src, dst_ref=halo.at[layer, pl.ds(PAD - r, r)],
            send_sem=send_sem.at[layer], recv_sem=recv_sem.at[layer],
            device_id=(ens, lax.rem(me + 1, n)), device_id_type=MESH)

    def source(layer):
        r = halo_rows(layer)
        return out_rows.at[layer, pl.ds(PAD - r, r)]

    @pl.when(jnp.logical_not(last))
    def _():
        pl.semaphore_wait(barrier, 1)

    ready = set()

    def once(key, copies):
        if key not in ready:
            ready.add(key)
            for c in copies:
                c.wait()

    def start_send(layer):
        @pl.when(jnp.logical_not(last))
        def _():
            halo_send(layer, source(layer)).start()

    def keep_rows(layer):
        r = halo_rows(layer)
        out_rows[layer, pl.ds(PAD - r, r), :] = h[pl.ds(PAD + rows - r, r), :]

    def z_item(layer, tile):
        s, k = where_of(layer)
        d = dilation(layer)
        base = PAD + tile * TILE
        if layer == 0:
            for t in (tile, tile - 1):
                if t >= 0:
                    once(("x", t), [x_copies[t]])
            once("b", small_copies[:1])
            if tile == tiles - 1:
                keep_rows(0)
                start_send(0)
        group = group_of[layer]
        if ("w", group) not in ready:
            once(("w", group), w_copies[group])
            if group + 1 < len(groups):
                for c in w_copies[group + 1]:
                    c.start()
        if tile == 0:
            r = halo_rows(layer)

            @pl.when(jnp.logical_not(first))
            def _():
                halo_send(layer, source(layer)).wait_recv()
            got = halo[layer, pl.ds(PAD - r, r), :]
            h[pl.ds(PAD - r, r), :] = jnp.where(first, jnp.zeros_like(got), got)
        now = h[pl.ds(base, TILE), :]
        if d % 16 == 0:
            past = h[pl.ds(base - d, TILE), :]
        else:
            wide = h[pl.ds(base - 16, TILE + 16), :].astype(F32)
            past = wide[16 - d:16 - d + TILE].astype(BF16)
        z = jnp.dot(jnp.concatenate([past, now], axis=1), wz[layer], preferred_element_type=F32)
        t = jnp.tanh(z[:, :gate] + b[s, pl.ds(k, 1), pl.ds(0, gate)])
        u = jnp.tanh(z[:, gate:] * 0.5 + b[s, pl.ds(k, 1), pl.ds(gate, gate)] * 0.5)
        g = ((t * 0.5) * (u + 1.0)).astype(BF16)
        spot = pl.ds(tile * TILE, TILE)
        g_all[spot, pl.ds(layer * gate, gate)] = g
        new = (now.astype(F32) + jnp.dot(g, wr[layer], preferred_element_type=F32)).astype(BF16)
        if layer + 1 == layers:
            hout[spot, :] = new
        else:
            h[pl.ds(base, TILE), :] = new
        if layer + 1 < layers and tile == tiles - 1:
            keep_rows(layer + 1)
            start_send(layer + 1)

    started = set()

    def s_item(pair, begin, end, final):
        spot = pl.ds(min(pair) * TILE, 2 * TILE)
        v = jnp.dot(g_all[spot, pl.ds(begin * gate, (end - begin) * gate)],
                    ws[pl.ds(begin, end - begin)].reshape((end - begin) * gate, skip.shape[1]),
                    preferred_element_type=F32)
        if pair in started:
            v = skip[spot, :] + v
        started.add(pair)
        if not final:
            skip[spot, :] = v
            return
        once("head", small_copies[1:])
        a = jnp.maximum(v, 0.0).astype(BF16)
        m = jnp.maximum(jnp.dot(a, w1[...], preferred_element_type=F32) + c1[...], 0.0).astype(BF16)
        y[spot, :] = jnp.dot(m, w2[...], preferred_element_type=F32) + c2[...]

    for item in program_of(layers, tiles, cycle):
        if item[0] == "z":
            z_item(*item[1:])
        else:
            s_item(*item[1:])

    @pl.when(jnp.logical_not(last))
    def _():
        for layer in range(layers):
            halo_send(layer, source(layer)).wait_send()


def solution(mesh):
    n = mesh.shape["sp"]
    row_spec = P(("ens", "sp"), None)

    def local_stack(x_seq, w_past, w_now, b_conv, w_res, w_skip, w_out1, b_out1, w_out2, b_out2):
        stacks, cycle, res, _ = w_past.shape
        gate = b_conv.shape[-1] // 2
        skip_ch = w_skip.shape[-1]
        classes = w_out2.shape[-1]
        rows = x_seq.shape[0]
        layers = stacks * cycle
        tiles = rows // TILE
        args = (x_seq, w_past, w_now, b_conv, w_res, w_skip, w_out1, b_out1.reshape(1, -1), w_out2,
                b_out2.reshape(1, -1))
        args = [pltpu.with_memory_space_constraint(a, pltpu.HBM) for a in args]
        vmem = pl.BlockSpec(memory_space=pltpu.VMEM)
        return pl.pallas_call(
            functools.partial(kernel, n, stacks, cycle),
            out_shape=(jax.ShapeDtypeStruct((rows, classes), F32),
                       jax.ShapeDtypeStruct((rows, res), BF16)),
            in_specs=[pl.BlockSpec(memory_space=pl.ANY)] * 10,
            out_specs=(vmem, vmem),
            scratch_shapes=[
                pltpu.VMEM((PAD + rows, res), BF16),
                pltpu.VMEM((rows, skip_ch), F32),
                pltpu.VMEM((rows, layers * gate), BF16),
                pltpu.VMEM((layers, 2 * res, 2 * gate), BF16),
                pltpu.VMEM((layers,) + w_res.shape[2:], BF16),
                pltpu.VMEM((layers,) + w_skip.shape[2:], BF16),
                pltpu.VMEM(b_conv.shape, F32),
                pltpu.VMEM(w_out1.shape, BF16),
                pltpu.VMEM((1, skip_ch), F32),
                pltpu.VMEM(w_out2.shape, BF16),
                pltpu.VMEM((1, classes), F32),
                pltpu.VMEM((layers, PAD, res), BF16),
                pltpu.VMEM((layers, PAD, res), BF16),
                pltpu.SemaphoreType.DMA((tiles,)),
                pltpu.SemaphoreType.DMA((len(group_bounds(layers, cycle)),)),
                pltpu.SemaphoreType.DMA((5,)),
                pltpu.SemaphoreType.DMA((layers,)),
                pltpu.SemaphoreType.DMA((layers,)),
            ],
            compiler_params=pltpu.CompilerParams(
                collective_id=0, has_side_effects=True, vmem_limit_bytes=48 * 1024 * 1024),
            name="stack",
        )(*args)

    return jax.shard_map(
        local_stack,
        mesh=mesh,
        in_specs=(row_spec, P(), P(), P(), P(), P(), P(), P(), P(), P()),
        out_specs=(row_spec, row_spec),
        check_vma=False,
    )
```

time: 130 us -> 41.4 us (0.32)
  starting transfers between devices: 67.1 us -> 0 us
  matrix products: 41.6 us -> 0 us
  Pallas kernels: 0 us -> 38.7 us
  waiting for transfers between devices: 9.67 us -> 0 us
  other arithmetic: 7.07 us -> 0 us
    ppermute x16 -> x0, starting transfers between devices: 67.1 us -> none  [local_stack(): halo_rows = lax.ppermute(hidden[-dilation:], 'sp', perm=shift_perm)]
    dot_general x65 -> x0, matrix products: 41.6 us -> none  [the longest x16 13.7 us: local_stack(): jnp.dot(shifted, w_past[stack_idx, layer_pos], preferred_element_type=jnp...]
    pallas_call x0 -> x1, Pallas kernels: none -> 38.7 us  [local_stack(): pl.pallas_call(functools.partial(kernel, n, stacks, cycle), out_shape=(ja...]
    ppermute x16 -> x0, waiting for transfers between devices: 9.67 us -> none  [local_stack(): halo_rows = lax.ppermute(hidden[-dilation:], 'sp', perm=shift_perm)]
    convert_element_type x16 -> x0, other arithmetic: 7.07 us -> none  [local_stack(): (jnp.tanh(pre_act[:, :gate_ch]) * jax.nn.sigmoid(pre_act[:, gate_ch:])).a...]
    slice x27 -> x0, local copies, waits for them, and re-layouts: 1.58 us -> none  [the longest x16 0.89 us: local_stack(): halo_rows = lax.ppermute(hidden[-dilation:], 'sp', perm=shift_perm)]
  transfers between devices with their start and end apart: 16 -> 0, of which waited for: 15 -> 0; matrix products, arithmetic and copies ran while one was open for 6% -> 0% of each run, Pallas kernels for 0% -> 0%
where the time goes in v2:
time: 41.4 us; the launch traced here: 41.2 us
  Pallas kernels  38.7 us (93%)
  local copies, waits for them, and re-layouts  1.94 us (5%)
  between operations  0.64 us (2%)
    pallas_call x1, Pallas kernels, local_stack(): pl.pallas_call(functools.partial(kernel, n, stacks, cycle), out_shape=(ja...  38.7 us
    unnamed x2, local copies, waits for them, and re-layouts  1.94 us

profile of v2, /device:TPU:113, one launch (start us, length us, event | category | flops | bytes accessed | tf_op | source)
XLA Modules:
  0.0 41.2 jit_solution(18386387814203583128)
XLA Ops:
  0.6 38.7 %stack.1 = (f32[1024,256]{1,0:T(8,128)S(1)}, bf16[1024,512]{1,0:T(8,128)(2,1)S(1)}) custom-call(bf16[1024,512]{1,0:T(8,128)(2,1)} %x_hbm.1, bf16[2,8,512,512]{3,2,1,0:T(8,128)(2,1)} %wp_hbm.1, bf16[2,8,512,512]{3,2,1,0:T(8,128)(2,1)} %wn_hbm.1, f32[2,8,512]{2,1,0:T(8,128)} %b_hbm.1, bf16[2,8,256,512]{3,2,1,0:T(8,128)(2,1)} %wr_hbm.1, ...), custom_call_target="tpu_custom_call" | custom-call | tf_op jit(solution)/shard_map/stack/pallas_call | solution.py:220
  39.3 1.0 %copy.14 = f32[1024,256]{1,0:T(8,128)} copy(f32[1024,256]{1,0:T(8,128)S(1)} %get-tuple-element.4) | data formatting | bytes 2097152
  40.3 1.0 %copy.15 = bf16[1024,512]{1,0:T(8,128)(2,1)} copy(bf16[1024,512]{1,0:T(8,128)(2,1)S(1)} %get-tuple-element.5) | data formatting | bytes 2097152

commit v3 on v2

v3 whole, which is shorter than its diff:
```python
import functools

import jax
import jax.numpy as jnp
from jax import lax
from jax.experimental import pallas as pl
from jax.experimental.pallas import tpu as pltpu
from jax.sharding import PartitionSpec as P

TILE = 256
PAD = 128
JOINT = 5
LAGS = (5, 3, 2, 0)
MESH = pl.DeviceIdType.MESH
F32 = jnp.float32
BF16 = jnp.bfloat16


def program_of(layers, tiles, cycle):
    steps = sorted((tiles * layer + LAGS[tile], layer, tile) for layer in range(layers) for tile in range(tiles))
    items = [("z", layer, tile) for _, layer, tile in steps]
    hi, lo = (tiles - 1, tiles - 2), (tiles - 3, tiles - 4)
    half, end = cycle - 2, layers - 1
    at = items.index(("z", cycle - 2, 0))
    items[at:at] = [("s", hi, 0, half), ("s", lo, 0, half)]
    at = items.index(("z", layers - 1, 0))
    items[at:at] = [("s", hi, half, end), ("s", lo, half, end)]
    return items


def group_bounds(layers, cycle):
    cuts = [0, 1, 3, 5]
    while cuts[-1] < layers:
        cuts.append(min(cuts[-1] + (3 if cuts[-1] <= cycle else 5), layers))
    return list(zip(cuts[:-1], cuts[1:]))


def kernel(n, stacks, cycle, x_hbm, wp_hbm, wn_hbm, b_hbm, wr_hbm, ws_hbm, w1_hbm, c1_hbm, w2_hbm, c2_hbm,
           hout, skip, g_last, ws_last, w1, c1, w2, c2, h, g_all, wz, wr, ws, b, halo, out_rows,
           x_sem, w_sem, small_sem, send_sem, recv_sem):
    rows, res = x_hbm.shape
    gate = wr_hbm.shape[2]
    layers = stacks * cycle
    tiles = rows // TILE
    me = lax.axis_index("sp")
    ens = lax.axis_index("ens")
    first = me == 0
    joint = min(JOINT, cycle)

    barrier = pltpu.get_barrier_semaphore()

    pl.semaphore_signal(barrier, inc=1, device_id=(ens, lax.rem(me + n - 1, n)), device_id_type=MESH)

    def where_of(layer):
        return layer // cycle, layer % cycle

    def dilation(layer):
        return 2 ** (layer % cycle)

    def halo_rows(layer):
        k = layer % cycle
        if k == 0:
            return 2 ** joint
        return 0 if k < joint else dilation(layer)

    def extra_rows(layer):
        k = layer % cycle
        need = sum(2 ** j for j in range(k + 1, joint))
        return -(-need // 16) * 16

    x_copies = [pltpu.make_async_copy(
        x_hbm.at[pl.ds(tile * TILE, TILE)], h.at[pl.ds(PAD + tile * TILE, TILE)], x_sem.at[tile])
        for tile in range(tiles)]
    groups = group_bounds(layers, cycle)
    group_of = {layer: i for i, (lo, hi) in enumerate(groups) for layer in range(lo, hi)}
    w_copies = []
    for i, (lo, hi) in enumerate(groups):
        s, k = where_of(lo)
        span = pl.ds(k, hi - lo)
        sem = w_sem.at[i]
        w_copies.append([
            pltpu.make_async_copy(wp_hbm.at[s, span], wz.at[pl.ds(lo, hi - lo), pl.ds(0, res)], sem),
            pltpu.make_async_copy(wn_hbm.at[s, span], wz.at[pl.ds(lo, hi - lo), pl.ds(res, res)], sem),
            pltpu.make_async_copy(wr_hbm.at[s, span], wr.at[pl.ds(lo, hi - lo)], sem),
            pltpu.make_async_copy(ws_hbm.at[s, span], ws.at[pl.ds(lo, hi - lo)], sem)])
    small_copies = [pltpu.make_async_copy(src, dst, small_sem.at[i]) for i, (src, dst) in enumerate(
        ((b_hbm, b), (w1_hbm, w1), (c1_hbm, c1), (w2_hbm, w2), (c2_hbm, c2), (ws_hbm.at[stacks - 1, cycle - 1], ws_last)))]
    x_copies[-1].start()
    small_copies[0].start()
    for c in w_copies[0]:
        c.start()
    for c in reversed(x_copies[:-1]):
        c.start()
    for c in w_copies[1]:
        c.start(priority=1)

    def halo_send(layer, src):
        r = halo_rows(layer)
        return pltpu.make_async_remote_copy(
            src_ref=src, dst_ref=halo.at[layer, pl.ds(PAD - r, r)],
            send_sem=send_sem.at[layer], recv_sem=recv_sem.at[layer],
            device_id=(ens, lax.rem(me + 1, n)), device_id_type=MESH)

    def source(layer):
        r = halo_rows(layer)
        return out_rows.at[layer, pl.ds(PAD - r, r)]

    halo[layers, :, :] = jnp.zeros(halo.shape[1:], BF16)
    pl.semaphore_wait(barrier, 1)

    ready = set()

    def once(key, copies):
        if key not in ready:
            ready.add(key)
            for c in copies:
                c.wait()

    def start_send(layer):
        halo_send(layer, source(layer)).start()

    def keep_rows(layer):
        r = halo_rows(layer)
        out_rows[layer, pl.ds(PAD - r, r), :] = h[pl.ds(PAD + rows - r, r), :]

    def z_item(layer, tile):
        s, k = where_of(layer)
        d = dilation(layer)
        base = PAD + tile * TILE
        if layer == 0:
            for t in (tile, tile - 1):
                if t >= 0:
                    once(("x", t), [x_copies[t]])
            once("b", small_copies[:1])
            if tile == tiles - 1:
                keep_rows(0)
                start_send(0)
        group = group_of[layer]
        if ("w", group) not in ready:
            once(("w", group), w_copies[group])
            if 1 < group + 1 < len(groups):
                for c in w_copies[group + 1]:
                    c.start(priority=1)
            if group + 1 == len(groups):
                for c in small_copies[1:]:
                    c.start(priority=1)
        r = halo_rows(layer)
        if tile == 0 and r:
            @pl.when(jnp.logical_not(first))
            def _():
                halo_send(layer, source(layer)).wait_recv()
            slot = layer + (layers - layer) * ((n - me) // n)
            h[pl.ds(PAD - r, r), :] = halo[slot, pl.ds(PAD - r, r), :]
        extra = extra_rows(layer) if tile == 0 else 0
        start, size = base - extra, TILE + extra
        now = h[pl.ds(start, size), :]
        if d % 16 == 0:
            past = h[pl.ds(start - d, size), :]
        else:
            wide = h[pl.ds(start - 16, size + 16), :].astype(F32)
            past = wide[16 - d:16 - d + size].astype(BF16)
        z = jnp.dot(jnp.concatenate([past, now], axis=1), wz[layer], preferred_element_type=F32)
        t = jnp.tanh(z[:, :gate] + b[s, pl.ds(k, 1), pl.ds(0, gate)])
        u = jnp.tanh(z[:, gate:] * 0.5 + b[s, pl.ds(k, 1), pl.ds(gate, gate)] * 0.5)
        g = ((t * 0.5) * (u + 1.0)).astype(BF16)
        spot = pl.ds(tile * TILE, TILE)
        if layer + 1 == layers:
            g_last[spot, :] = g
        else:
            g_all[layer, spot, :] = g[extra:]
        new = (now.astype(F32) + jnp.dot(g, wr[layer], preferred_element_type=F32)).astype(BF16)
        if layer + 1 == layers:
            hout[spot, :] = new
        else:
            h[pl.ds(base, TILE), :] = new[extra:]
        if extra:
            h[pl.ds(start, extra), :] = jnp.where(first, jnp.zeros_like(new[:extra]), new[:extra])
        if layer + 1 < layers and tile == tiles - 1 and halo_rows(layer + 1):
            keep_rows(layer + 1)
            start_send(layer + 1)

    started = set()

    def s_item(pair, begin, end):
        spot = pl.ds(min(pair) * TILE, 2 * TILE)
        v = jnp.dot(jnp.concatenate([g_all[layer, spot, :] for layer in range(begin, end)], axis=1),
                    ws[pl.ds(begin, end - begin)].reshape((end - begin) * gate, skip.shape[1]),
                    preferred_element_type=F32)
        if pair in started:
            v = skip[spot, :] + v
        started.add(pair)
        skip[spot, :] = v

    for item in program_of(layers, tiles, cycle):
        if item[0] == "z":
            z_item(*item[1:])
        else:
            s_item(*item[1:])

    for c in small_copies[1:]:
        c.wait()
    exchanges = [layer for layer in range(layers) if halo_rows(layer)]
    for layer in exchanges:
        halo_send(layer, source(layer)).wait_send()

    @pl.when(first)
    def _():
        for layer in exchanges:
            halo_send(layer, source(layer)).wait_recv()


def head(h, skip, g, ws, w1, c1, w2, c2, y_hbm, hout_hbm, y, h_sem, y_sem):
    tiles = y.shape[0] // TILE
    h_copy = pltpu.make_async_copy(h, hout_hbm, h_sem)
    h_copy.start()
    copies = []
    for tile in range(tiles):
        spot = pl.ds(tile * TILE, TILE)
        v = skip[spot, :] + jnp.dot(g[spot, :], ws[...], preferred_element_type=F32)
        a = jnp.maximum(v, 0.0).astype(BF16)
        m = jnp.maximum(jnp.dot(a, w1[...], preferred_element_type=F32) + c1[...], 0.0).astype(BF16)
        y[spot, :] = jnp.dot(m, w2[...], preferred_element_type=F32) + c2[...]
        copies.append(pltpu.make_async_copy(y.at[spot], y_hbm.at[spot], y_sem.at[tile]))
        if tile % 2:
            for c in copies[-2:]:
                c.start()
    h_copy.wait()
    for c in copies:
        c.wait()


def solution(mesh):
    n = mesh.shape["sp"]
    row_spec = P(("ens", "sp"), None)

    def local_stack(x_seq, w_past, w_now, b_conv, w_res, w_skip, w_out1, b_out1, w_out2, b_out2):
        stacks, cycle, res, _ = w_past.shape
        gate = b_conv.shape[-1] // 2
        skip_ch = w_skip.shape[-1]
        classes = w_out2.shape[-1]
        rows = x_seq.shape[0]
        layers = stacks * cycle
        tiles = rows // TILE
        args = (x_seq, w_past, w_now, b_conv, w_res, w_skip, w_out1, b_out1.reshape(1, -1), w_out2,
                b_out2.reshape(1, -1))
        args = [pltpu.with_memory_space_constraint(a, pltpu.HBM) for a in args]
        vmem = pl.BlockSpec(memory_space=pltpu.VMEM)
        anywhere = pl.BlockSpec(memory_space=pl.ANY)
        parts = pl.pallas_call(
            functools.partial(kernel, n, stacks, cycle),
            out_shape=(jax.ShapeDtypeStruct((rows, res), BF16),
                       jax.ShapeDtypeStruct((rows, skip_ch), F32),
                       jax.ShapeDtypeStruct((rows, gate), BF16),
                       jax.ShapeDtypeStruct((gate, skip_ch), BF16),
                       jax.ShapeDtypeStruct(w_out1.shape, BF16),
                       jax.ShapeDtypeStruct((1, skip_ch), F32),
                       jax.ShapeDtypeStruct(w_out2.shape, BF16),
                       jax.ShapeDtypeStruct((1, classes), F32)),
            in_specs=[anywhere] * 10,
            out_specs=(vmem,) * 8,
            scratch_shapes=[
                pltpu.VMEM((PAD + rows, res), BF16),
                pltpu.VMEM((layers - 1, rows, gate), BF16),
                pltpu.VMEM((layers, 2 * res, 2 * gate), BF16),
                pltpu.VMEM((layers,) + w_res.shape[2:], BF16),
                pltpu.VMEM((layers,) + w_skip.shape[2:], BF16),
                pltpu.VMEM(b_conv.shape, F32),
                pltpu.VMEM((layers + 1, PAD, res), BF16),
                pltpu.VMEM((layers, PAD, res), BF16),
                pltpu.SemaphoreType.DMA((tiles,)),
                pltpu.SemaphoreType.DMA((len(group_bounds(layers, cycle)),)),
                pltpu.SemaphoreType.DMA((6,)),
                pltpu.SemaphoreType.DMA((layers,)),
                pltpu.SemaphoreType.DMA((layers,)),
            ],
            compiler_params=pltpu.CompilerParams(
                collective_id=0, has_side_effects=True, vmem_limit_bytes=48 * 1024 * 1024),
            name="stack",
        )(*args)
        return pl.pallas_call(
            head,
            out_shape=(jax.ShapeDtypeStruct((rows, classes), F32), jax.ShapeDtypeStruct((rows, res), BF16)),
            in_specs=[vmem] * 8,
            out_specs=(anywhere, anywhere),
            scratch_shapes=[pltpu.VMEM((rows, classes), F32), pltpu.SemaphoreType.DMA,
                            pltpu.SemaphoreType.DMA((tiles,))],
            compiler_params=pltpu.CompilerParams(vmem_limit_bytes=16 * 1024 * 1024),
            name="head",
        )(*parts)

    return jax.shard_map(
        local_stack,
        mesh=mesh,
        in_specs=(row_spec, P(), P(), P(), P(), P(), P(), P(), P(), P()),
        out_specs=(row_spec, row_spec),
        check_vma=False,
    )
```

time: 41.4 us -> 39.8 us (0.961)
  local copies, waits for them, and re-layouts: 1.94 us -> 0 us
    unnamed x2 -> x0, local copies, waits for them, and re-layouts: 1.94 us -> none
    pallas_call x0 -> x1, Pallas kernels: none -> 1.86 us  [local_stack(): pl.pallas_call(head, out_shape=(jax.ShapeDtypeStruct((rows, classes), F32...]
    pallas_call x1, Pallas kernels: 38.7 us -> 37.1 us  [local_stack(): pl.pallas_call(functools.partial(kernel, n, stacks, cycle), out_shape=(ja...]
where the time goes in v3:
time: 39.8 us
  Pallas kernels  38.9 us (98%)
  between operations  0.8 us (2%)
    pallas_call x1, Pallas kernels, local_stack(): pl.pallas_call(functools.partial(kernel, n, stacks, cycle), out_shape=(ja...  37.1 us
    pallas_call x1, Pallas kernels, local_stack(): pl.pallas_call(head, out_shape=(jax.ShapeDtypeStruct((rows, classes), F32...  1.86 us

profile of v3, /device:TPU:113, one launch (start us, length us, event | category | flops | bytes accessed | tf_op | source)
XLA Modules:
  0.0 39.8 jit_solution(13532656223164502868)
XLA Ops:
  0.6 37.1 %stack.1 = (bf16[1024,512]{1,0:T(8,128)(2,1)S(1)}, f32[1024,256]{1,0:T(8,128)S(1)}, bf16[1024,256]{1,0:T(8,128)(2,1)S(1)}, bf16[256,256]{1,0:T(8,128)(2,1)S(1)},...) custom-call(bf16[1024,512]{1,0:T(8,128)(2,1)} %x_hbm.1, ...), custom_call_target="tpu_custom_call" | custom-call | tf_op jit(solution)/shard_map/stack/pallas_call | solution.py:249
  37.7 1.9 %head.1 = (f32[1024,256]{1,0:T(8,128)}, bf16[1024,512]{1,0:T(8,128)(2,1)}) custom-call(bf16[1024,512]{1,0:T(8,128)(2,1)S(1)} %get-tuple-element.10.h, f32[1024,256]{1,0:T(8,128)S(1)} %get-tuple-element.11.skip, bf16[1024,256]{1,0:T(8,128)(2,1)S(1)} %get-tuple-element.12.g, bf16[256,256]{1,0:T(8,128)(2,1)S(1)} %get-tuple-element.13.ws, ...), custom_call_target="tpu_custom_call" | custom-call | tf_op jit(solution)/shard_map/head/pallas_call | solution.py:280

commit v4 on v3

--- a/solution.py
+++ b/solution.py
@@ -7,10 +7,10 @@
 from jax.experimental.pallas import tpu as pltpu
 from jax.sharding import PartitionSpec as P
 
-TILE = 256
+TILE = 512
 PAD = 128
 JOINT = 5
-LAGS = (5, 3, 2, 0)
+LAGS = (1, 0)
 MESH = pl.DeviceIdType.MESH
 F32 = jnp.float32
 BF16 = jnp.bfloat16
@@ -19,12 +19,12 @@
 def program_of(layers, tiles, cycle):
     steps = sorted((tiles * layer + LAGS[tile], layer, tile) for layer in range(layers) for tile in range(tiles))
     items = [("z", layer, tile) for _, layer, tile in steps]
-    hi, lo = (tiles - 1, tiles - 2), (tiles - 3, tiles - 4)
+    hi = (1, 0)
     half, end = cycle - 2, layers - 1
     at = items.index(("z", cycle - 2, 0))
-    items[at:at] = [("s", hi, 0, half), ("s", lo, 0, half)]
+    items[at:at] = [("s", hi, 0, half)]
     at = items.index(("z", layers - 1, 0))
-    items[at:at] = [("s", hi, half, end), ("s", lo, half, end)]
+    items[at:at] = [("s", hi, half, end)]
     return items
 
 
@@ -159,7 +159,8 @@
         else:
             wide = h[pl.ds(start - 16, size + 16), :].astype(F32)
             past = wide[16 - d:16 - d + size].astype(BF16)
-        z = jnp.dot(jnp.concatenate([past, now], axis=1), wz[layer], preferred_element_type=F32)
+        z = (jnp.dot(past, wz[layer, pl.ds(0, res)], preferred_element_type=F32)
+             + jnp.dot(now, wz[layer, pl.ds(res, res)], preferred_element_type=F32))
         t = jnp.tanh(z[:, :gate] + b[s, pl.ds(k, 1), pl.ds(0, gate)])
         u = jnp.tanh(z[:, gate:] * 0.5 + b[s, pl.ds(k, 1), pl.ds(gate, gate)] * 0.5)
         g = ((t * 0.5) * (u + 1.0)).astype(BF16)

time: 39.8 us -> 36.9 us (0.927)
  Pallas kernels: 38.9 us -> 35.9 us
    pallas_call x1, Pallas kernels: 37.1 us -> 34.1 us  [local_stack(): pl.pallas_call(functools.partial(kernel, n, stacks, cycle), out_shape=(ja...]
where the time goes in v4:
time: 36.9 us; the launch traced here: 36.7 us
  Pallas kernels  35.9 us (97%)
  between operations  0.8 us (2%)
    pallas_call x1, Pallas kernels, local_stack(): pl.pallas_call(functools.partial(kernel, n, stacks, cycle), out_shape=(ja...  34.1 us
    pallas_call x1, Pallas kernels, local_stack(): pl.pallas_call(head, out_shape=(jax.ShapeDtypeStruct((rows, classes), F32...  1.78 us

profile of v4, /device:TPU:113, one launch (start us, length us, event | category | flops | bytes accessed | tf_op | source)
XLA Modules:
  0.0 36.7 jit_solution(14023924447790757844)
XLA Ops:
  0.6 34.1 %stack.1 = (bf16[1024,512]{1,0:T(8,128)(2,1)S(1)}, f32[1024,256]{1,0:T(8,128)S(1)}, bf16[1024,256]{1,0:T(8,128)(2,1)S(1)}, bf16[256,256]{1,0:T(8,128)(2,1)S(1)},...) custom-call(bf16[1024,512]{1,0:T(8,128)(2,1)} %x_hbm.1, ...), custom_call_target="tpu_custom_call" | custom-call | tf_op jit(solution)/shard_map/stack/pallas_call | solution.py:250
  34.8 1.8 %head.1 = (f32[1024,256]{1,0:T(8,128)}, bf16[1024,512]{1,0:T(8,128)(2,1)}) custom-call(bf16[1024,512]{1,0:T(8,128)(2,1)S(1)} %get-tuple-element.10.h, f32[1024,256]{1,0:T(8,128)S(1)} %get-tuple-element.11.skip, bf16[1024,256]{1,0:T(8,128)(2,1)S(1)} %get-tuple-element.12.g, bf16[256,256]{1,0:T(8,128)(2,1)S(1)} %get-tuple-element.13.ws, ...), custom_call_target="tpu_custom_call" | custom-call | tf_op jit(solution)/shard_map/head/pallas_call | solution.py:281
